TPU v7x, 32 devices: a whole 2x2x4 slice. The times are simulated.
32 devices in a mesh: expert: 4 (over x, core), rows: 8 (over z, y).
Axes of the slice: x: 2, y: 2, z: 4, core: 2. Of those that a mesh axis runs over, the one named last changes fastest.
Arguments:
- step: int32 [], replicated, may hold values from 2 to 8
- gradient: bfloat16 [4, 4096, 14336], P('expert', 'rows'), may hold values from -8 to 8
- weight: bfloat16 [4, 4096, 14336], P('expert', 'rows'), may hold values from -0.119628906 to 0.119628906
- row_state: float32 [4, 4096], P('expert', 'rows'), may hold values from 0.3 to 3
- col_state: float32 [4, 14336], P('expert', 'rows'), may hold values from 0.3 to 3
- prev_msq: float32 [4, 8], P('expert', 'rows'), may hold values from 2 to 500
Outputs:
- new_weight: bfloat16 [4, 4096, 14336], P('expert', 'rows')
- new_row_state: float32 [4, 4096], P('expert', 'rows')
- new_col_state: float32 [4, 14336], P('expert', 'rows')
- new_msq: float32 [4, 8], P('expert', 'rows')
All inputs are finite; a program needn't handle non-finite values.
Results may differ from a plain program's by a relative error of at most 0.001.
Values sent between devices are 32-bit elements; how exact they have to be, the bound alone decides.
A program may use at most 128 MiB of HBM per device.

v0:
```python
import functools

import jax
import jax.numpy as jnp
from jax import lax
from jax.experimental import pallas as pl
from jax.experimental.pallas import tpu as pltpu
from jax.sharding import PartitionSpec as P

MESH = pl.DeviceIdType.MESH
RATE = 0.01
TINY = 1e-30
LANES = 128
ROWS = 16
UNROLL = 4


def lane_sum(x):
    total = x[:, :LANES]
    for k in range(1, x.shape[1] // LANES):
        total = total + x[:, k * LANES : (k + 1) * LANES]
    return total


def statistics_kernel(
    n, experts, step_ref, prev_ref, row_hbm, col_hbm, g_hbm, w_hbm,
    g_out, w_out, scale_out, factor_out, new_row_out, new_col_out,
    acc, part, parts_in, message, messages_in, clip_out, clips_in,
    row_ref, col_ref, small_sem, g_sem, w_sem, clip_send, clip_recv, part_send, part_recv, gather_send, gather_recv,
):
    me = lax.axis_index("rows")
    mine = lax.axis_index("expert")
    rows, columns = g_out.shape
    width = columns // n

    def column_slice(c):
        return pl.ds(pl.multiple_of(c * width, LANES), width)

    def partner(k):
        peer, bit = 0, 1
        while bit < n:
            peer = peer + bit * ((me // bit + k // bit) % 2)
            bit *= 2
        return peer

    def chunk_of(s):
        return partner(n - 1 - s)

    def g_copy(s):
        cols = column_slice(chunk_of(s))
        return pltpu.make_async_copy(g_hbm.at[:, cols], g_out.at[:, cols], g_sem.at[s])

    def w_copy(s):
        cols = column_slice(s)
        return pltpu.make_async_copy(w_hbm.at[:, cols], w_out.at[:, cols], w_sem.at[s])

    def clip_copy(k):
        peer = lax.rem(mine + k, experts)
        return pltpu.make_async_remote_copy(
            src_ref=clip_out, dst_ref=clips_in.at[k - 1], send_sem=clip_send.at[k - 1],
            recv_sem=clip_recv.at[k - 1], device_id={"expert": peer}, device_id_type=MESH,
        )

    def part_copy(s):
        c = chunk_of(s)
        return pltpu.make_async_remote_copy(
            src_ref=part.at[s], dst_ref=parts_in.at[s], send_sem=part_send.at[s],
            recv_sem=part_recv.at[s], device_id={"rows": c}, device_id_type=MESH,
        )

    def gather_copy(k):
        peer = partner(k)
        return pltpu.make_async_remote_copy(
            src_ref=message, dst_ref=messages_in.at[k - 1], send_sem=gather_send.at[k - 1],
            recv_sem=gather_recv.at[k - 1], device_id={"rows": peer}, device_id_type=MESH,
        )

    pairs = ((row_hbm, row_ref), (col_hbm, col_ref))
    small = [pltpu.make_async_copy(src, dst, small_sem.at[k]) for k, (src, dst) in enumerate(pairs)]
    for copy in small:
        copy.start()
    for s in range(n):
        g_copy(s).start()

    barrier = pltpu.get_barrier_semaphore()
    for k in range(1, n):
        pl.semaphore_signal(barrier, inc=1, device_id={"rows": lax.rem(me + k, n)}, device_id_type=MESH)
    for k in range(1, experts):
        pl.semaphore_signal(barrier, inc=1, device_id={"expert": lax.rem(mine + k, experts)}, device_id_type=MESH)

    acc[...] = jnp.zeros_like(acc)
    for copy in small:
        copy.wait()
    clip_out[...] = jnp.full((1, LANES), prev_ref[0], jnp.float32)
    beta = 1.0 - jnp.exp(-0.8 * jnp.log(jnp.full((1, LANES), step_ref[0], jnp.int32).astype(jnp.float32)))

    def chunk(s):
        cols = column_slice(chunk_of(s))
        g_copy(s).wait()

        def body(i, carry):
            at = pl.ds(pl.multiple_of(i * ROWS, ROWS), ROWS)
            x = g_out[at, cols].astype(jnp.float32)
            squares = x * x
            acc[at, :] += lane_sum(squares)
            return carry + (squares[: ROWS // 2] + squares[ROWS // 2 :])

        col = lax.fori_loop(0, rows // ROWS, body, jnp.zeros((ROWS // 2, width), jnp.float32), unroll=UNROLL)
        part[s] = jnp.sum(col, axis=0, keepdims=True)

    half = n // 2

    @pl.loop(0, half)
    def _(s):
        chunk(s)

    pl.semaphore_wait(barrier, n - 1 + experts - 1)
    for k in range(1, experts):
        clip_copy(k).start()
    for s in range(half):
        part_copy(s).start()

    @pl.loop(half, n - 1)
    def _(s):
        w_copy(s - half).start(priority=1)
        chunk(s)
        part_copy(s).start()

    for s in range(n - 1 - half, n):
        w_copy(s).start(priority=1)
    chunk(n - 1)

    share = lane_sum(row_ref[...]) * beta
    share = share + (1.0 - beta) * (jnp.sum(acc[...], axis=0, keepdims=True) * (1.0 / columns) + TINY * (rows / LANES))
    clips = clip_out[...]
    for k in range(1, experts):
        clip_copy(k).wait()
        clips = clips + clips_in[k - 1]
    total = part[n - 1]
    for s in range(n - 1):
        part_copy(s).wait()
        total = total + parts_in[s]
    beta_cols = jnp.concatenate([beta] * (width // LANES), axis=1)
    new_col = beta_cols * col_ref[...] + (1.0 - beta_cols) * (total * (1.0 / (rows * n)) + TINY)
    message[:, :width] = new_col
    message[:, width : width + LANES] = share
    message[:, width + LANES :] = clips
    for k in reversed(range(1, n)):
        gather_copy(k).start()

    new_col_out[...] = new_col
    sums = jnp.sum(jnp.transpose(acc[...]), axis=0, keepdims=True)
    beta_rows = jnp.concatenate([beta] * (rows // LANES), axis=1)
    new_row = beta_rows * row_ref[...] + (1.0 - beta_rows) * (sums * (1.0 / columns) + TINY)
    new_row_out[...] = new_row
    scale_out[...] = jnp.transpose(jnp.broadcast_to(lax.rsqrt(new_row), (LANES, rows)))
    for s in range(n):
        w_copy(s).wait()

    for k in reversed(range(1, n)):
        gather_copy(k).wait()
        share = share + messages_in[k - 1, :, width : width + LANES]
        clips = clips + messages_in[k - 1, :, width + LANES :]
    row_mean = jnp.sum(share, axis=1, keepdims=True) * (1.0 / (rows * n))
    clip_square = clips[:, :1] * (1.0 / (n * experts))
    common = RATE * jnp.sqrt(row_mean) * lax.rsqrt(clip_square)
    factor_out[:, column_slice(me)] = lax.rsqrt(new_col) * common
    for k in range(1, n):
        factor_out[:, column_slice(partner(k))] = lax.rsqrt(messages_in[k - 1, :, :width]) * common


def update_kernel(
    block, g_ref, w_ref, scale_ref, factor_ref, row_ref, col_ref,
    new_w_hbm, new_row_out, new_col_out, msq_out, stage, sem,
):
    rows, columns = g_ref.shape
    blocks = columns // block

    def out_copy(b):
        cols = pl.ds(pl.multiple_of(b * block, LANES), block)
        return pltpu.make_async_copy(stage.at[b % 2], new_w_hbm.at[:, cols], sem.at[b % 2])

    new_row_out[...] = row_ref[...]
    new_col_out[...] = col_ref[...]

    def do_block(b, total):
        cols = pl.ds(pl.multiple_of(b * block, LANES), block)
        slot = b % 2

        @pl.when(b >= 2)
        def _():
            out_copy(b - 2).wait()

        factor = jnp.broadcast_to(factor_ref[:, cols], (ROWS, block))

        def body(i, total):
            at = pl.ds(pl.multiple_of(i * ROWS, ROWS), ROWS)
            scale = jnp.concatenate([scale_ref[at, :]] * (block // LANES), axis=1)
            move = g_ref[at, cols].astype(jnp.float32) * factor * scale
            stage[slot, at, :] = (w_ref[at, cols].astype(jnp.float32) - move).astype(jnp.bfloat16)
            return total + lane_sum(move * move)

        total = lax.fori_loop(0, rows // ROWS, body, total, unroll=UNROLL)
        out_copy(b).start()
        return total

    total = lax.fori_loop(0, blocks, do_block, jnp.zeros((ROWS, LANES), jnp.float32))
    for b in range(max(blocks - 2, 0), blocks):
        out_copy(b).wait()
    msq = jnp.sum(jnp.sum(total, axis=0, keepdims=True), axis=1, keepdims=True)
    msq_out[...] = msq * (1.0 / (RATE * RATE * rows * columns))


def block_width(columns):
    tiles = columns // LANES
    for d in (8, 7, 4, 2, 1):
        if tiles % d == 0:
            return d * LANES


def shards(step, gradient, weight, row_state, col_state, prev_msq):
    _, rows, columns = gradient.shape
    n = lax.axis_size("rows")
    experts = lax.axis_size("expert")
    width = columns // n
    f32, bf16 = jnp.float32, gradient.dtype
    vmem = pl.BlockSpec(memory_space=pltpu.VMEM)
    hbm = pl.BlockSpec(memory_space=pltpu.HBM)
    dma = pltpu.SemaphoreType.DMA
    big = rows * columns * 2
    g, w, scale, factor, new_row, new_col = pl.pallas_call(
        functools.partial(statistics_kernel, n, experts),
        out_shape=[
            pltpu.VMEM((rows, columns), bf16),
            pltpu.VMEM((rows, columns), bf16),
            pltpu.VMEM((rows, LANES), f32),
            pltpu.VMEM((1, columns), f32),
            pltpu.VMEM((1, rows), f32),
            pltpu.VMEM((1, width), f32),
        ],
        in_specs=[pl.BlockSpec(memory_space=pltpu.SMEM)] * 2 + [hbm] * 4,
        out_specs=[vmem] * 6,
        scratch_shapes=[
            pltpu.VMEM((rows, LANES), f32),
            pltpu.VMEM((n, 1, width), f32),
            pltpu.VMEM((n - 1, 1, width), f32),
            pltpu.VMEM((1, width + 2 * LANES), f32),
            pltpu.VMEM((n - 1, 1, width + 2 * LANES), f32),
            pltpu.VMEM((1, LANES), f32),
            pltpu.VMEM((experts - 1, 1, LANES), f32),
            pltpu.VMEM((1, rows), f32),
            pltpu.VMEM((1, width), f32),
            dma((2,)), dma((n,)), dma((n,)), dma((experts - 1,)), dma((experts - 1,)),
            dma((n - 1,)), dma((n - 1,)), dma((n - 1,)), dma((n - 1,)),
        ],
        compiler_params=pltpu.CompilerParams(
            collective_id=0, has_side_effects=True, vmem_limit_bytes=8 * 2**20
        ),
        name="statistics",
    )(
        step.reshape(1), prev_msq.reshape(1),
        *(
            pltpu.with_memory_space_constraint(x, pltpu.HBM)
            for x in (row_state, col_state, gradient.reshape(rows, columns), weight.reshape(rows, columns))
        )
    )
    block = block_width(columns)
    new_weight, new_row, new_col, msq = pl.pallas_call(
        functools.partial(update_kernel, block),
        out_shape=[
            jax.ShapeDtypeStruct((rows, columns), bf16),
            jax.ShapeDtypeStruct((1, rows), f32),
            jax.ShapeDtypeStruct((1, width), f32),
            jax.ShapeDtypeStruct((1, 1), f32),
        ],
        in_specs=[vmem] * 6,
        out_specs=[hbm, vmem, vmem, vmem],
        scratch_shapes=[pltpu.VMEM((2, rows, block), bf16), dma((2,))],
        compiler_params=pltpu.CompilerParams(vmem_limit_bytes=8 * 2**20),
        name="update",
    )(g, w, scale, factor, new_row, new_col)
    return (new_weight.reshape(1, rows, columns), new_row, new_col, msq)


def solution(mesh):
    split = P("expert", "rows")
    whole = P("expert", "rows", None)
    return jax.shard_map(
        shards,
        mesh=mesh,
        in_specs=(P(), whole, whole, split, split, split),
        out_specs=(whole, split, split, split),
        check_vma=False,
    )
```

profile of v0, /device:TPU:0, one launch (start us, length us, event | category | flops | bytes accessed | tf_op | source)
XLA Modules:
  0.0 32.9 jit_solution(4597859387281616469)
XLA Ops:
  1.9 18.9 %statistics.1 = (bf16[512,14336]{1,0:T(8,128)(2,1)S(1)}, bf16[512,14336]{1,0:T(8,128)(2,1)S(1)}, f32[512,128]{1,0:T(8,128)S(1)}, f32[1,14336]{1,0:T(1,128)S(1)},...) custom-call(s32[1]{0:T(128)} %bitcast.5.step_ref, f32[1]{0:T(128)} %bitcast.6.prev_ref, f32[1,512]{1,0:T(1,128)} %row_hbm.1, ...), custom_call_target="tpu_custom_call" | custom-call | tf_op jit(solution)/shard_map/statistics/pallas_call | solution.py:231
  20.9 12.0 %update.1 = (bf16[512,14336]{1,0:T(8,128)(2,1)}, f32[1,512]{1,0:T(1,128)}, f32[1,1792]{1,0:T(1,128)}, f32[1,1]{1,0:T(1,128)}) custom-call(bf16[512,14336]{1,0:T(8,128)(2,1)S(1)} %get-tuple-element.14.g_ref, bf16[512,14336]{1,0:T(8,128)(2,1)S(1)} %get-tuple-element.15.w_ref, f32[512,128]{1,0:T(8,128)S(1)} %get-tuple-element.16.scale_ref, ...), custom_call_target="tpu_custom_call" | custom-call | tf_op jit(solution)/shard_map/update/pallas_call | solution.py:268
where the time goes:
time: 33.1 us; the launch traced here: 32.9 us
  Pallas kernels  31 us (94%)
  between operations  1.93 us (6%)
    pallas_call x1, Pallas kernels, shards(): pl.pallas_call(functools.partial(statistics_kernel, n, experts), out_shap...  18.9 us
    pallas_call x1, Pallas kernels, shards(): pl.pallas_call(functools.partial(update_kernel, block), out_shape=[jax.Sh...  12 us

commit v1 on v0

--- a/solution.py
+++ b/solution.py
@@ -13,6 +13,7 @@
 LANES = 128
 ROWS = 16
 UNROLL = 4
+SLOTS = 4
 
 
 def lane_sum(x):
@@ -23,14 +24,15 @@
 
 
 def statistics_kernel(
-    n, experts, step_ref, prev_ref, row_hbm, col_hbm, g_hbm, w_hbm,
-    g_out, w_out, scale_out, factor_out, new_row_out, new_col_out,
-    acc, part, parts_in, message, messages_in, clip_out, clips_in,
-    row_ref, col_ref, small_sem, g_sem, w_sem, clip_send, clip_recv, part_send, part_recv, gather_send, gather_recv,
+    n, experts, early, step_ref, prev_ref, row_hbm, col_hbm, g_hbm, w_hbm,
+    u_out, w_out, factor_out, new_row_out, new_col_out, msq_out,
+    acc, scale_ref, energy, part, parts_in, message, messages_in, clip_out, clips_in,
+    row_ref, col_ref, small_sem, g_sem, w_sem,
+    clip_send, clip_recv, part_send, part_recv, gather_send, gather_recv,
 ):
     me = lax.axis_index("rows")
     mine = lax.axis_index("expert")
-    rows, columns = g_out.shape
+    rows, columns = u_out.shape
     width = columns // n
 
     def column_slice(c):
@@ -48,7 +50,7 @@
 
     def g_copy(s):
         cols = column_slice(chunk_of(s))
-        return pltpu.make_async_copy(g_hbm.at[:, cols], g_out.at[:, cols], g_sem.at[s])
+        return pltpu.make_async_copy(g_hbm.at[:, cols], w_out.at[:, cols], g_sem.at[s])
 
     def w_copy(s):
         cols = column_slice(s)
@@ -100,13 +102,28 @@
 
         def body(i, carry):
             at = pl.ds(pl.multiple_of(i * ROWS, ROWS), ROWS)
-            x = g_out[at, cols].astype(jnp.float32)
+            x = w_out[at, cols].astype(jnp.float32)
+            u_out[at, cols] = x
             squares = x * x
             acc[at, :] += lane_sum(squares)
             return carry + (squares[: ROWS // 2] + squares[ROWS // 2 :])
 
         col = lax.fori_loop(0, rows // ROWS, body, jnp.zeros((ROWS // 2, width), jnp.float32), unroll=UNROLL)
         part[s] = jnp.sum(col, axis=0, keepdims=True)
+
+    def scaled(s):
+        cols = column_slice(s)
+
+        def body(i, carry):
+            at = pl.ds(pl.multiple_of(i * ROWS, ROWS), ROWS)
+            scale = jnp.concatenate([scale_ref[at, :]] * (width // LANES), axis=1)
+            u = u_out[at, cols] * scale
+            u_out[at, cols] = u
+            squares = u * u
+            return carry + (squares[: ROWS // 2] + squares[ROWS // 2 :])
+
+        col = lax.fori_loop(0, rows // ROWS, body, jnp.zeros((ROWS // 2, width), jnp.float32), unroll=2)
+        energy[:, cols] = jnp.sum(col, axis=0, keepdims=True)
 
     half = n // 2
 
@@ -122,16 +139,24 @@
 
     @pl.loop(half, n - 1)
     def _(s):
-        w_copy(s - half).start(priority=1)
         chunk(s)
         part_copy(s).start()
 
-    for s in range(n - 1 - half, n):
-        w_copy(s).start(priority=1)
     chunk(n - 1)
-
-    share = lane_sum(row_ref[...]) * beta
-    share = share + (1.0 - beta) * (jnp.sum(acc[...], axis=0, keepdims=True) * (1.0 / columns) + TINY * (rows / LANES))
+    for s in range(n):
+        w_copy(s).start()
+
+    beta_rows = jnp.concatenate([beta] * (rows // LANES), axis=1)
+    sums = jnp.sum(jnp.transpose(acc[...]), axis=0, keepdims=True)
+    new_row = beta_rows * row_ref[...] + (1.0 - beta_rows) * (sums * (1.0 / columns) + TINY)
+    new_row_out[...] = new_row
+    scale_ref[...] = jnp.transpose(jnp.broadcast_to(lax.rsqrt(new_row), (LANES, rows)))
+    share = lane_sum(new_row)
+
+    @pl.loop(0, early)
+    def _(s):
+        scaled(s)
+
     clips = clip_out[...]
     for k in range(1, experts):
         clip_copy(k).wait()
@@ -147,13 +172,12 @@
     message[:, width + LANES :] = clips
     for k in reversed(range(1, n)):
         gather_copy(k).start()
-
     new_col_out[...] = new_col
-    sums = jnp.sum(jnp.transpose(acc[...]), axis=0, keepdims=True)
-    beta_rows = jnp.concatenate([beta] * (rows // LANES), axis=1)
-    new_row = beta_rows * row_ref[...] + (1.0 - beta_rows) * (sums * (1.0 / columns) + TINY)
-    new_row_out[...] = new_row
-    scale_out[...] = jnp.transpose(jnp.broadcast_to(lax.rsqrt(new_row), (LANES, rows)))
+
+    @pl.loop(early, n)
+    def _(s):
+        scaled(s)
+
     for s in range(n):
         w_copy(s).wait()
 
@@ -164,51 +188,52 @@
     row_mean = jnp.sum(share, axis=1, keepdims=True) * (1.0 / (rows * n))
     clip_square = clips[:, :1] * (1.0 / (n * experts))
     common = RATE * jnp.sqrt(row_mean) * lax.rsqrt(clip_square)
-    factor_out[:, column_slice(me)] = lax.rsqrt(new_col) * common
-    for k in range(1, n):
-        factor_out[:, column_slice(partner(k))] = lax.rsqrt(messages_in[k - 1, :, :width]) * common
+    moved = jnp.zeros((1, LANES), jnp.float32)
+    for k in range(n):
+        cols = column_slice(partner(k))
+        column = new_col if k == 0 else messages_in[k - 1, :, :width]
+        factor = lax.rsqrt(column) * common
+        factor_out[:, cols] = factor
+        moved = moved + lane_sum(energy[:, cols] * (factor * factor))
+    msq_out[...] = moved * (1.0 / (RATE * RATE * rows * columns))
 
 
 def update_kernel(
-    block, g_ref, w_ref, scale_ref, factor_ref, row_ref, col_ref,
+    block, u_ref, w_ref, factor_ref, row_ref, col_ref, msq_ref,
     new_w_hbm, new_row_out, new_col_out, msq_out, stage, sem,
 ):
-    rows, columns = g_ref.shape
+    rows, columns = u_ref.shape
     blocks = columns // block
 
     def out_copy(b):
+        slot = lax.rem(b, SLOTS)
         cols = pl.ds(pl.multiple_of(b * block, LANES), block)
-        return pltpu.make_async_copy(stage.at[b % 2], new_w_hbm.at[:, cols], sem.at[b % 2])
+        return pltpu.make_async_copy(stage.at[slot], new_w_hbm.at[:, cols], sem.at[slot])
+
+    @pl.loop(0, blocks)
+    def _(b):
+        cols = pl.ds(pl.multiple_of(b * block, LANES), block)
+        slot = lax.rem(b, SLOTS)
+
+        @pl.when(b >= SLOTS)
+        def _():
+            out_copy(b - SLOTS).wait()
+
+        factor = jnp.broadcast_to(factor_ref[:, cols], (ROWS, block))
+
+        @pl.loop(0, rows // ROWS, unroll=UNROLL)
+        def _(i):
+            at = pl.ds(pl.multiple_of(i * ROWS, ROWS), ROWS)
+            new = w_ref[at, cols].astype(jnp.float32) - u_ref[at, cols] * factor
+            stage[slot, at, :] = new.astype(jnp.bfloat16)
+
+        out_copy(b).start()
 
     new_row_out[...] = row_ref[...]
     new_col_out[...] = col_ref[...]
-
-    def do_block(b, total):
-        cols = pl.ds(pl.multiple_of(b * block, LANES), block)
-        slot = b % 2
-
-        @pl.when(b >= 2)
-        def _():
-            out_copy(b - 2).wait()
-
-        factor = jnp.broadcast_to(factor_ref[:, cols], (ROWS, block))
-
-        def body(i, total):
-            at = pl.ds(pl.multiple_of(i * ROWS, ROWS), ROWS)
-            scale = jnp.concatenate([scale_ref[at, :]] * (block // LANES), axis=1)
-            move = g_ref[at, cols].astype(jnp.float32) * factor * scale
-            stage[slot, at, :] = (w_ref[at, cols].astype(jnp.float32) - move).astype(jnp.bfloat16)
-            return total + lane_sum(move * move)
-
-        total = lax.fori_loop(0, rows // ROWS, body, total, unroll=UNROLL)
-        out_copy(b).start()
-        return total
-
-    total = lax.fori_loop(0, blocks, do_block, jnp.zeros((ROWS, LANES), jnp.float32))
-    for b in range(max(blocks - 2, 0), blocks):
+    msq_out[...] = jnp.sum(msq_ref[...], axis=1, keepdims=True)
+    for b in range(max(blocks - SLOTS, 0), blocks):
         out_copy(b).wait()
-    msq = jnp.sum(jnp.sum(total, axis=0, keepdims=True), axis=1, keepdims=True)
-    msq_out[...] = msq * (1.0 / (RATE * RATE * rows * columns))
 
 
 def block_width(columns):
@@ -227,21 +252,22 @@
     vmem = pl.BlockSpec(memory_space=pltpu.VMEM)
     hbm = pl.BlockSpec(memory_space=pltpu.HBM)
     dma = pltpu.SemaphoreType.DMA
-    big = rows * columns * 2
-    g, w, scale, factor, new_row, new_col = pl.pallas_call(
-        functools.partial(statistics_kernel, n, experts),
+    u, w, factor, new_row, new_col, msq = pl.pallas_call(
+        functools.partial(statistics_kernel, n, experts, n // 4),
         out_shape=[
+            pltpu.VMEM((rows, columns), f32),
             pltpu.VMEM((rows, columns), bf16),
-            pltpu.VMEM((rows, columns), bf16),
-            pltpu.VMEM((rows, LANES), f32),
             pltpu.VMEM((1, columns), f32),
             pltpu.VMEM((1, rows), f32),
             pltpu.VMEM((1, width), f32),
+            pltpu.VMEM((1, LANES), f32),
         ],
         in_specs=[pl.BlockSpec(memory_space=pltpu.SMEM)] * 2 + [hbm] * 4,
         out_specs=[vmem] * 6,
         scratch_shapes=[
             pltpu.VMEM((rows, LANES), f32),
+            pltpu.VMEM((rows, LANES), f32),
+            pltpu.VMEM((1, columns), f32),
             pltpu.VMEM((n, 1, width), f32),
             pltpu.VMEM((n - 1, 1, width), f32),
             pltpu.VMEM((1, width + 2 * LANES), f32),
@@ -261,8 +287,11 @@
         step.reshape(1), prev_msq.reshape(1),
         *(
             pltpu.with_memory_space_constraint(x, pltpu.HBM)
-            for x in (row_state, col_state, gradient.reshape(rows, columns), weight.reshape(rows, columns))
-        )
+            for x in (
+                row_state, col_state,
+                gradient.reshape(rows, columns), weight.reshape(rows, columns),
+            )
+        ),
     )
     block = block_width(columns)
     new_weight, new_row, new_col, msq = pl.pallas_call(
@@ -275,10 +304,10 @@
         ],
         in_specs=[vmem] * 6,
         out_specs=[hbm, vmem, vmem, vmem],
-        scratch_shapes=[pltpu.VMEM((2, rows, block), bf16), dma((2,))],
+        scratch_shapes=[pltpu.VMEM((SLOTS, rows, block), bf16), dma((SLOTS,))],
         compiler_params=pltpu.CompilerParams(vmem_limit_bytes=8 * 2**20),
         name="update",
-    )(g, w, scale, factor, new_row, new_col)
+    )(u, w, factor, new_row, new_col, msq)
     return (new_weight.reshape(1, rows, columns), new_row, new_col, msq)
 
 

time: 33.1 us -> 27.9 us (0.84)
  Pallas kernels: 31 us -> 25.8 us
    pallas_call x1, Pallas kernels: 12 us -> 6.37 us  [shards(): pl.pallas_call(functools.partial(update_kernel, block), out_shape=[jax.Sh...]
    pallas_call x1, Pallas kernels: 18.9 us -> 19.4 us  [shards(): pl.pallas_call(functools.partial(statistics_kernel, n, experts, n // 4),...]
where the time goes in v1:
time: 27.9 us; the launch traced here: 27.7 us
  Pallas kernels  25.8 us (92%)
  between operations  1.93 us (7%)
    pallas_call x1, Pallas kernels, shards(): pl.pallas_call(functools.partial(statistics_kernel, n, experts, n // 4),...  19.4 us
    pallas_call x1, Pallas kernels, shards(): pl.pallas_call(functools.partial(update_kernel, block), out_shape=[jax.Sh...  6.37 us

profile of v1, /device:TPU:0, one launch (start us, length us, event | category | flops | bytes accessed | tf_op | source)
XLA Modules:
  0.0 27.7 jit_solution(3566032170251567190)
XLA Ops:
  1.9 19.4 %statistics.1 = (f32[512,14336]{1,0:T(8,128)S(1)}, bf16[512,14336]{1,0:T(8,128)(2,1)S(1)}, f32[1,14336]{1,0:T(1,128)S(1)}, f32[1,512]{1,0:T(1,128)S(1)}, f32[1,1792]{1,0:T(1,128)S(1)}, /*index=5*/f32[1,128]{1,0:T(1,128)S(1)}) custom-call(s32[1]{0:T(128)} %bitcast.5.step_ref, f32[1]{0:T(128)} %bitcast.6.prev_ref, f32[1,512]{1,0:T(1,128)} %row_hbm.1, ...), custom_call_target="tpu_custom_call" | custom-call | tf_op jit(solution)/shard_map/statistics/pallas_call | solution.py:255
  21.4 6.4 %update.1 = (bf16[512,14336]{1,0:T(8,128)(2,1)}, f32[1,512]{1,0:T(1,128)}, f32[1,1792]{1,0:T(1,128)}, f32[1,1]{1,0:T(1,128)}) custom-call(f32[512,14336]{1,0:T(8,128)S(1)} %get-tuple-element.14.u_ref, bf16[512,14336]{1,0:T(8,128)(2,1)S(1)} %get-tuple-element.15.w_ref, f32[1,14336]{1,0:T(1,128)S(1)} %get-tuple-element.16.factor_ref, ...), custom_call_target="tpu_custom_call" | custom-call | tf_op jit(solution)/shard_map/update/pallas_call | solution.py:297

commit v2 on v1

v2 whole, which is shorter than its diff:
```python
import functools

import jax
import jax.numpy as jnp
from jax import lax
from jax.experimental import pallas as pl
from jax.experimental.pallas import tpu as pltpu
from jax.sharding import PartitionSpec as P

MESH = pl.DeviceIdType.MESH
RATE = 0.01
TINY = 1e-30
LANES = 128
ROWS = 16
BLOCK = 128
DEPTH = 4
EARLY = 2
SLOTS = 4
ROW = [slice(r, r + ROWS) for r in range(0, BLOCK, ROWS)]
TILE = [slice(k * LANES, (k + 1) * LANES) for k in range(16)]


def lane_sum(x):
    total = x[:, :LANES]
    for k in range(1, x.shape[1] // LANES):
        total = total + x[:, k * LANES : (k + 1) * LANES]
    return total


def statistics_kernel(
    n, experts, step_ref, prev_ref, row_hbm, col_hbm, g_hbm, w_hbm,
    u_out, w_out, factor_out, common_out, new_row_out, new_col_out, moved_out,
    acc, scale_ref, energy, part, parts_in, message, messages_in, clip_out, clips_in,
    row_ref, col_ref, small_sem, g_sem, w_sem,
    clip_send, clip_recv, part_send, part_recv, gather_send, gather_recv,
):
    me = lax.axis_index("rows")
    mine = lax.axis_index("expert")
    rows, columns = u_out.shape
    width = columns // n

    def column_slice(c):
        return pl.ds(pl.multiple_of(c * width, LANES), width)

    tiles = tile_count(width)

    def strip_slice(c, first):
        return pl.ds(pl.multiple_of(c * width + first * LANES, LANES), tiles * LANES)

    def partner(k):
        peer, bit = 0, 1
        while bit < n:
            peer = peer + bit * ((me // bit + k // bit) % 2)
            bit *= 2
        return peer

    def chunk_of(s):
        return partner(n - 1 - s)

    def g_copy(s):
        cols = column_slice(chunk_of(s))
        return pltpu.make_async_copy(g_hbm.at[:, cols], w_out.at[:, cols], g_sem.at[lax.rem(s, DEPTH)])

    def w_copy(s):
        cols = column_slice(s)
        return pltpu.make_async_copy(w_hbm.at[:, cols], w_out.at[:, cols], w_sem)

    def clip_copy(k):
        peer = lax.rem(mine + k, experts)
        return pltpu.make_async_remote_copy(
            src_ref=clip_out, dst_ref=clips_in.at[k - 1], send_sem=clip_send,
            recv_sem=clip_recv, device_id={"expert": peer}, device_id_type=MESH,
        )

    def part_copy(s):
        c = chunk_of(s)
        return pltpu.make_async_remote_copy(
            src_ref=part.at[s], dst_ref=parts_in.at[s], send_sem=part_send,
            recv_sem=part_recv, device_id={"rows": c}, device_id_type=MESH,
        )

    def gather_copy(k):
        peer = partner(k)
        return pltpu.make_async_remote_copy(
            src_ref=message, dst_ref=messages_in.at[k - 1], send_sem=gather_send,
            recv_sem=gather_recv.at[k - 1], device_id={"rows": peer}, device_id_type=MESH,
        )

    pairs = ((row_hbm, row_ref), (col_hbm, col_ref))
    small = [pltpu.make_async_copy(src, dst, small_sem.at[k]) for k, (src, dst) in enumerate(pairs)]
    for copy in small:
        copy.start()
    for s in range(DEPTH):
        g_copy(s).start()

    barrier = pltpu.get_barrier_semaphore()
    for k in range(1, n):
        pl.semaphore_signal(barrier, inc=1, device_id={"rows": lax.rem(me + k, n)}, device_id_type=MESH)
    for k in range(1, experts):
        pl.semaphore_signal(barrier, inc=1, device_id={"expert": lax.rem(mine + k, experts)}, device_id_type=MESH)

    clip_out[...] = jnp.full((1, LANES), prev_ref[0], jnp.float32)
    beta = 1.0 - jnp.exp(-0.8 * jnp.log(jnp.full((1, LANES), step_ref[0], jnp.int32).astype(jnp.float32)))

    def chunk(s):
        for first in range(0, width // LANES, tiles):
            strip = strip_slice(chunk_of(s), first)

            def body(i, carry):
                at = pl.ds(pl.multiple_of(i * BLOCK, BLOCK), BLOCK)
                source, target = w_out.at[at, strip], u_out.at[at, strip]
                carry = list(carry)
                for row in ROW:
                    for k in range(tiles):
                        x = source[row, TILE[k]].astype(jnp.float32)
                        target[row, TILE[k]] = x
                        squares = x * x
                        carry[k] = carry[k] + (squares[: ROWS // 2] + squares[ROWS // 2 :])
                return tuple(carry)

            zeros = (jnp.zeros((ROWS // 2, LANES), jnp.float32),) * tiles
            col = lax.fori_loop(0, rows // BLOCK, body, zeros)
            for k in range(tiles):
                part[s, :, (first + k) * LANES : (first + k + 1) * LANES] = jnp.sum(col[k], axis=0, keepdims=True)

    def scaled(s):
        for first in range(0, width // LANES, tiles):
            strip = strip_slice(s, first)

            def body(i, carry):
                at = pl.ds(pl.multiple_of(i * BLOCK, BLOCK), BLOCK)
                target, scales = u_out.at[at, strip], scale_ref.at[at]
                carry = list(carry)
                for row in ROW:
                    scale = scales[row, :]
                    for k in range(tiles):
                        u = target[row, TILE[k]] * scale
                        target[row, TILE[k]] = u
                        squares = u * u
                        carry[k] = carry[k] + (squares[: ROWS // 2] + squares[ROWS // 2 :])
                return tuple(carry)

            zeros = (jnp.zeros((ROWS // 2, LANES), jnp.float32),) * tiles
            col = lax.fori_loop(0, rows // BLOCK, body, zeros)
            for k in range(tiles):
                energy.at[:, strip][:, TILE[k]] = jnp.sum(col[k], axis=0, keepdims=True)

    half = n // 2

    @pl.loop(0, half)
    def _(s):
        g_copy(s).wait()
        g_copy(s + DEPTH).start()
        chunk(s)

    pl.semaphore_wait(barrier, n - 1 + experts - 1)
    for k in range(1, experts):
        clip_copy(k).start()
    for s in range(half):
        part_copy(s).start()

    @pl.loop(half, n - 1)
    def _(s):
        g_copy(s).wait()

        @pl.when(s + DEPTH < n)
        def _():
            g_copy(s + DEPTH).start()

        @pl.when(s + DEPTH >= n)
        def _():
            w_copy(chunk_of(s + DEPTH - n)).start()

        chunk(s)
        part_copy(s).start()

    g_copy(n - 1).wait()
    for s in range(DEPTH - 1, n - 1):
        w_copy(chunk_of(s)).start()
    chunk(n - 1)
    w_copy(chunk_of(n - 1)).start()

    for copy in small:
        copy.wait()
    beta_rows = jnp.concatenate([beta] * (rows // LANES), axis=1)
    squares = part[0]
    for s in range(1, n):
        squares = squares + part[s]
    share = lane_sum(row_ref[...]) * beta
    share = share + (1.0 - beta) * (lane_sum(squares) * (1.0 / columns) + TINY * (rows / LANES))
    share = jnp.broadcast_to(jnp.sum(share, axis=1, keepdims=True), (1, LANES))

    def whole_copy(ref, send, recv):
        return pltpu.make_async_remote_copy(
            src_ref=ref, dst_ref=ref, send_sem=send, recv_sem=recv,
            device_id={"rows": partner(1)}, device_id_type=MESH,
        )

    def respond():
        clips = clip_out[...]
        whole_copy(clips_in, clip_send, clip_recv).wait()
        for k in range(1, experts):
            clips = clips + clips_in[k - 1]
        whole_copy(parts_in, part_send, part_recv).wait_recv()
        total = part[n - 1]
        for s in range(n - 1):
            total = total + parts_in[s]
        beta_cols = jnp.concatenate([beta] * (width // LANES), axis=1)
        message[:, :width] = beta_cols * col_ref[...] + (1.0 - beta_cols) * (total * (1.0 / (rows * n)) + TINY)
        message[:, width : width + LANES] = share
        message[:, width + LANES :] = clips
        for k in reversed(range(1, n)):
            gather_copy(k).start()

    def row_sums(i):
        at = pl.ds(pl.multiple_of(i * ROWS, ROWS), ROWS)
        source = u_out.at[at]
        sums = [None] * 4
        for k in range(columns // LANES):
            x = source[:, k * LANES : (k + 1) * LANES]
            sums[k % 4] = x * x if k < 4 else sums[k % 4] + x * x
        acc[at, :] = (sums[0] + sums[1]) + (sums[2] + sums[3])

    middle = rows // ROWS // 2

    @pl.loop(0, middle)
    def _(i):
        row_sums(i)

    @pl.when(me != 0)
    def _():
        respond()

    @pl.loop(middle, rows // ROWS)
    def _(i):
        row_sums(i)

    sums = jnp.sum(jnp.transpose(acc[...]), axis=0, keepdims=True)
    new_row = beta_rows * row_ref[...] + (1.0 - beta_rows) * (sums * (1.0 / columns) + TINY)
    new_row_out[...] = new_row
    scale_ref[...] = jnp.transpose(jnp.broadcast_to(lax.rsqrt(new_row), (LANES, rows)))
    early = jnp.where(me == 0, n * EARLY // 8, 0)

    @pl.loop(0, early)
    def _(s):
        scaled(s)

    @pl.when(me == 0)
    def _():
        respond()

    @pl.loop(early, n)
    def _(s):
        scaled(s)

    pltpu.make_async_copy(w_hbm, w_out, w_sem).wait()

    new_col_out[...] = message[:, :width]
    whole_copy(parts_in, part_send, part_recv).wait_send()
    share, clips, moved = 0.0, 0.0, 0.0
    for k in range(n):
        cols = column_slice(partner(k))
        if k > 0:
            gather_copy(k).wait_recv()
        got = message[...] if k == 0 else messages_in[k - 1]
        inverse = lax.rsqrt(got[:, :width])
        factor_out[:, cols] = inverse
        share = share + got[:, width : width + LANES]
        clips = clips + got[:, width + LANES :]
        moved = moved + lane_sum(energy[:, cols] * (inverse * inverse))
    whole_copy(messages_in, gather_send, gather_recv.at[0]).wait_send()
    common_out[...] = RATE * jnp.sqrt(share * (1.0 / (rows * n))) * lax.rsqrt(clips * (1.0 / (n * experts)))
    moved_out[...] = moved


def update_kernel(
    block, u_ref, w_ref, factor_ref, common_ref, row_ref, col_ref, moved_ref,
    new_w_hbm, new_row_hbm, new_col_hbm, msq_hbm, stage, msq_ref, sem, small_sem,
):
    rows, columns = u_ref.shape
    blocks = columns // block
    common = common_ref[...]
    msq = moved_ref[...] * (common * common) * (1.0 / (RATE * RATE * rows * columns))
    msq_ref[...] = jnp.sum(msq, axis=1, keepdims=True)

    def out_copy(b):
        slot = lax.rem(b, SLOTS)
        cols = pl.ds(pl.multiple_of(b * block, LANES), block)
        return pltpu.make_async_copy(stage.at[slot], new_w_hbm.at[:, cols], sem.at[slot])

    pairs = ((row_ref, new_row_hbm), (col_ref, new_col_hbm), (msq_ref, msq_hbm))
    small = [pltpu.make_async_copy(src, dst, small_sem.at[k]) for k, (src, dst) in enumerate(pairs)]

    @pl.loop(0, blocks)
    def _(b):
        slot = lax.rem(b, SLOTS)

        @pl.when(b >= SLOTS)
        def _():
            out_copy(b - SLOTS).wait()

        cols = pl.ds(pl.multiple_of(b * block, LANES), block)
        factor = [jnp.broadcast_to(factor_ref.at[:, cols][:, TILE[k]] * common, (ROWS, LANES)) for k in range(block // LANES)]

        @pl.loop(0, rows // BLOCK)
        def _(i):
            at = pl.ds(pl.multiple_of(i * BLOCK, BLOCK), BLOCK)
            w, u, target = w_ref.at[at, cols], u_ref.at[at, cols], stage.at[slot, at]
            for row in ROW:
                for k in range(block // LANES):
                    new = w[row, TILE[k]].astype(jnp.float32) - u[row, TILE[k]] * factor[k]
                    target[row, TILE[k]] = new.astype(jnp.bfloat16)

        out_copy(b).start()

        @pl.when(b == 0)
        def _():
            for copy in small:
                copy.start()

    for copy in small:
        copy.wait()
    for b in range(max(blocks - SLOTS, 0), blocks):
        out_copy(b).wait()


def tile_count(width):
    total = width // LANES
    for d in (14, 7, 8, 4, 2, 1):
        if total % d == 0:
            return d


def block_width(columns):
    tiles = columns // LANES
    for d in (8, 7, 4, 2, 1):
        if tiles % d == 0:
            return d * LANES


def shards(step, gradient, weight, row_state, col_state, prev_msq):
    _, rows, columns = gradient.shape
    n = lax.axis_size("rows")
    experts = lax.axis_size("expert")
    width = columns // n
    f32, bf16 = jnp.float32, gradient.dtype
    vmem = pl.BlockSpec(memory_space=pltpu.VMEM)
    hbm = pl.BlockSpec(memory_space=pltpu.HBM)
    dma = pltpu.SemaphoreType.DMA
    u, w, factor, common, new_row, new_col, moved = pl.pallas_call(
        functools.partial(statistics_kernel, n, experts),
        out_shape=[
            pltpu.VMEM((rows, columns), f32),
            pltpu.VMEM((rows, columns), bf16),
            pltpu.VMEM((1, columns), f32),
            pltpu.VMEM((1, LANES), f32),
            pltpu.VMEM((1, rows), f32),
            pltpu.VMEM((1, width), f32),
            pltpu.VMEM((1, LANES), f32),
        ],
        in_specs=[pl.BlockSpec(memory_space=pltpu.SMEM)] * 2 + [hbm] * 4,
        out_specs=[vmem] * 7,
        scratch_shapes=[
            pltpu.VMEM((rows, LANES), f32),
            pltpu.VMEM((rows, LANES), f32),
            pltpu.VMEM((1, columns), f32),
            pltpu.VMEM((n, 1, width), f32),
            pltpu.VMEM((n - 1, 1, width), f32),
            pltpu.VMEM((1, width + 2 * LANES), f32),
            pltpu.VMEM((n - 1, 1, width + 2 * LANES), f32),
            pltpu.VMEM((1, LANES), f32),
            pltpu.VMEM((experts - 1, 1, LANES), f32),
            pltpu.VMEM((1, rows), f32),
            pltpu.VMEM((1, width), f32),
            dma((2,)), dma((DEPTH,)), dma, dma, dma, dma, dma, dma, dma((n - 1,)),
        ],
        compiler_params=pltpu.CompilerParams(
            collective_id=0, has_side_effects=True, vmem_limit_bytes=8 * 2**20
        ),
        name="statistics",
    )(
        step.reshape(1), prev_msq.reshape(1),
        *(
            pltpu.with_memory_space_constraint(x, pltpu.HBM)
            for x in (
                row_state, col_state,
                gradient.reshape(rows, columns), weight.reshape(rows, columns),
            )
        ),
    )
    block = block_width(columns)
    new_weight, new_row, new_col, msq = pl.pallas_call(
        functools.partial(update_kernel, block),
        out_shape=[
            jax.ShapeDtypeStruct((rows, columns), bf16),
            jax.ShapeDtypeStruct((1, rows), f32),
            jax.ShapeDtypeStruct((1, width), f32),
            jax.ShapeDtypeStruct((1, 1), f32),
        ],
        in_specs=[vmem] * 7,
        out_specs=[hbm] * 4,
        scratch_shapes=[pltpu.VMEM((SLOTS, rows, block), bf16), pltpu.VMEM((1, 1), f32), dma((SLOTS,)), dma((3,))],
        compiler_params=pltpu.CompilerParams(vmem_limit_bytes=8 * 2**20),
        name="update",
    )(u, w, factor, common, new_row, new_col, moved)
    return (new_weight.reshape(1, rows, columns), new_row, new_col, msq)


def solution(mesh):
    split = P("expert", "rows")
    whole = P("expert", "rows", None)
    return jax.shard_map(
        shards,
        mesh=mesh,
        in_specs=(P(), whole, whole, split, split, split),
        out_specs=(whole, split, split, split),
        check_vma=False,
    )
```

time: 27.9 us -> 23.3 us (0.84)
  Pallas kernels: 25.8 us -> 21.2 us
    pallas_call x1, Pallas kernels: 19.4 us -> 15.6 us  [shards(): pl.pallas_call(functools.partial(statistics_kernel, n, experts), out_shap...]
    pallas_call x1, Pallas kernels: 6.37 us -> 5.64 us  [shards(): pl.pallas_call(functools.partial(update_kernel, block), out_shape=[jax.Sh...]
where the time goes in v2:
time: 23.3 us; the launch traced here: 23.1 us
  Pallas kernels  21.2 us (91%)
  between operations  1.93 us (8%)
    pallas_call x1, Pallas kernels, shards(): pl.pallas_call(functools.partial(statistics_kernel, n, experts), out_shap...  15.6 us
    pallas_call x1, Pallas kernels, shards(): pl.pallas_call(functools.partial(update_kernel, block), out_shape=[jax.Sh...  5.64 us

profile of v2, /device:TPU:0, one launch (start us, length us, event | category | flops | bytes accessed | tf_op | source)
XLA Modules:
  0.0 23.1 jit_solution(15681630798445443990)
XLA Ops:
  1.9 15.6 %statistics.1 = (f32[512,14336]{1,0:T(8,128)S(1)}, bf16[512,14336]{1,0:T(8,128)(2,1)S(1)}, f32[1,14336]{1,0:T(1,128)S(1)}, f32[1,128]{1,0:T(1,128)S(1)}, f32[1,5...) custom-call(s32[1]{0:T(128)} %bitcast.5.step_ref, f32[1]{0:T(128)} %bitcast.6.prev_ref, ...), custom_call_target="tpu_custom_call" | custom-call | tf_op jit(solution)/shard_map/statistics/pallas_call | solution.py:350
  17.5 5.6 %update.1 = (bf16[512,14336]{1,0:T(8,128)(2,1)}, f32[1,512]{1,0:T(1,128)}, f32[1,1792]{1,0:T(1,128)}, f32[1,1]{1,0:T(1,128)}) custom-call(f32[512,14336]{1,0:T(8,128)S(1)} %get-tuple-element.15.u_ref, bf16[512,14336]{1,0:T(8,128)(2,1)S(1)} %get-tuple-element.16.w_ref, f32[1,14336]{1,0:T(1,128)S(1)} %get-tuple-element.17.factor_ref, ...), custom_call_target="tpu_custom_call" | custom-call | tf_op jit(solution)/shard_map/update/pallas_call | solution.py:392

commit v3 on v2

--- a/solution.py
+++ b/solution.py
@@ -15,7 +15,7 @@
 BLOCK = 128
 DEPTH = 4
 EARLY = 2
-SLOTS = 4
+SLOTS = 8
 ROW = [slice(r, r + ROWS) for r in range(0, BLOCK, ROWS)]
 TILE = [slice(k * LANES, (k + 1) * LANES) for k in range(16)]
 
@@ -30,9 +30,9 @@
 def statistics_kernel(
     n, experts, step_ref, prev_ref, row_hbm, col_hbm, g_hbm, w_hbm,
     u_out, w_out, factor_out, common_out, new_row_out, new_col_out, moved_out,
-    acc, scale_ref, energy, part, parts_in, message, messages_in, clip_out, clips_in,
+    acc, scale_ref, energy, part, parts_in, raws_in, message, messages_in, clip_out, clips_in,
     row_ref, col_ref, small_sem, g_sem, w_sem,
-    clip_send, clip_recv, part_send, part_recv, gather_send, gather_recv,
+    clip_send, clip_recv, part_send, part_recv, raw_send, raw_recv, gather_send, gather_recv,
 ):
     me = lax.axis_index("rows")
     mine = lax.axis_index("expert")
@@ -77,6 +77,12 @@
         return pltpu.make_async_remote_copy(
             src_ref=part.at[s], dst_ref=parts_in.at[s], send_sem=part_send,
             recv_sem=part_recv, device_id={"rows": c}, device_id_type=MESH,
+        )
+
+    def raw_copy(s, k):
+        return pltpu.make_async_remote_copy(
+            src_ref=part.at[s], dst_ref=raws_in.at[n - 2 - s, k - 1], send_sem=raw_send,
+            recv_sem=raw_recv, device_id={"rows": partner(k)}, device_id_type=MESH,
         )
 
     def gather_copy(k):
@@ -145,34 +151,40 @@
             for k in range(tiles):
                 energy.at[:, strip][:, TILE[k]] = jnp.sum(col[k], axis=0, keepdims=True)
 
-    half = n // 2
-
-    @pl.loop(0, half)
+    ready = jnp.where(me == 0, n - 3, jnp.where(me >= n // 2, 1, n // 2))
+
+    @pl.loop(0, n - 1)
     def _(s):
         g_copy(s).wait()
-        g_copy(s + DEPTH).start()
+
+        @pl.when(s + DEPTH < n)
+        def _():
+            g_copy(s + DEPTH).start()
+
+        @pl.when(s + DEPTH >= n)
+        def _():
+            w_copy(chunk_of(s + DEPTH - n)).start()
+
         chunk(s)
 
-    pl.semaphore_wait(barrier, n - 1 + experts - 1)
-    for k in range(1, experts):
-        clip_copy(k).start()
-    for s in range(half):
-        part_copy(s).start()
-
-    @pl.loop(half, n - 1)
-    def _(s):
-        g_copy(s).wait()
-
-        @pl.when(s + DEPTH < n)
-        def _():
-            g_copy(s + DEPTH).start()
-
-        @pl.when(s + DEPTH >= n)
-        def _():
-            w_copy(chunk_of(s + DEPTH - n)).start()
-
-        chunk(s)
-        part_copy(s).start()
+        @pl.when(s + 1 == ready)
+        def _():
+            pl.semaphore_wait(barrier, n - 1 + experts - 1)
+            for k in range(1, experts):
+                clip_copy(k).start()
+
+            @pl.loop(0, s)
+            def _(t):
+                part_copy(t).start()
+
+        @pl.when(jnp.logical_and(s + 1 >= ready, s < n - 3))
+        def _():
+            part_copy(s).start()
+
+        @pl.when(s >= n - 3)
+        def _():
+            for k in reversed(range(1, n)):
+                raw_copy(s, k).start()
 
     g_copy(n - 1).wait()
     for s in range(DEPTH - 1, n - 1):
@@ -186,6 +198,8 @@
     squares = part[0]
     for s in range(1, n):
         squares = squares + part[s]
+    beta_cols = jnp.concatenate([beta] * (width // LANES), axis=1)
+    weight = (1.0 - beta_cols) * (1.0 / (rows * n))
     share = lane_sum(row_ref[...]) * beta
     share = share + (1.0 - beta) * (lane_sum(squares) * (1.0 / columns) + TINY * (rows / LANES))
     share = jnp.broadcast_to(jnp.sum(share, axis=1, keepdims=True), (1, LANES))
@@ -203,10 +217,9 @@
             clips = clips + clips_in[k - 1]
         whole_copy(parts_in, part_send, part_recv).wait_recv()
         total = part[n - 1]
-        for s in range(n - 1):
+        for s in range(n - 3):
             total = total + parts_in[s]
-        beta_cols = jnp.concatenate([beta] * (width // LANES), axis=1)
-        message[:, :width] = beta_cols * col_ref[...] + (1.0 - beta_cols) * (total * (1.0 / (rows * n)) + TINY)
+        message[:, :width] = beta_cols * col_ref[...] + (1.0 - beta_cols) * TINY + weight * total
         message[:, width : width + LANES] = share
         message[:, width + LANES :] = clips
         for k in reversed(range(1, n)):
@@ -255,15 +268,21 @@
 
     pltpu.make_async_copy(w_hbm, w_out, w_sem).wait()
 
-    new_col_out[...] = message[:, :width]
     whole_copy(parts_in, part_send, part_recv).wait_send()
+    whole_copy(raws_in, raw_send, raw_recv).wait()
     share, clips, moved = 0.0, 0.0, 0.0
     for k in range(n):
         cols = column_slice(partner(k))
         if k > 0:
             gather_copy(k).wait_recv()
         got = message[...] if k == 0 else messages_in[k - 1]
-        inverse = lax.rsqrt(got[:, :width])
+        raw = 0.0
+        for x in range(1, 3):
+            raw = raw + (part[n - 1 - x] if k == x else raws_in[x - 1, (k ^ x) - 1])
+        column = got[:, :width] + weight * raw
+        if k == 0:
+            new_col_out[...] = column
+        inverse = lax.rsqrt(column)
         factor_out[:, cols] = inverse
         share = share + got[:, width : width + LANES]
         clips = clips + got[:, width + LANES :]
@@ -302,14 +321,12 @@
         cols = pl.ds(pl.multiple_of(b * block, LANES), block)
         factor = [jnp.broadcast_to(factor_ref.at[:, cols][:, TILE[k]] * common, (ROWS, LANES)) for k in range(block // LANES)]
 
-        @pl.loop(0, rows // BLOCK)
-        def _(i):
-            at = pl.ds(pl.multiple_of(i * BLOCK, BLOCK), BLOCK)
-            w, u, target = w_ref.at[at, cols], u_ref.at[at, cols], stage.at[slot, at]
-            for row in ROW:
-                for k in range(block // LANES):
-                    new = w[row, TILE[k]].astype(jnp.float32) - u[row, TILE[k]] * factor[k]
-                    target[row, TILE[k]] = new.astype(jnp.bfloat16)
+        w, u = w_ref.at[:, cols], u_ref.at[:, cols]
+        for r in range(0, rows, ROWS):
+            row = slice(r, r + ROWS)
+            for k in range(block // LANES):
+                new = w[row, TILE[k]].astype(jnp.float32) - u[row, TILE[k]] * factor[k]
+                stage[slot, row, TILE[k]] = new.astype(jnp.bfloat16)
 
         out_copy(b).start()
 
@@ -333,7 +350,7 @@
 
 def block_width(columns):
     tiles = columns // LANES
-    for d in (8, 7, 4, 2, 1):
+    for d in (4, 2, 1):
         if tiles % d == 0:
             return d * LANES
 
@@ -365,14 +382,15 @@
             pltpu.VMEM((rows, LANES), f32),
             pltpu.VMEM((1, columns), f32),
             pltpu.VMEM((n, 1, width), f32),
-            pltpu.VMEM((n - 1, 1, width), f32),
+            pltpu.VMEM((n - 3, 1, width), f32),
+            pltpu.VMEM((2, n - 1, 1, width), f32),
             pltpu.VMEM((1, width + 2 * LANES), f32),
             pltpu.VMEM((n - 1, 1, width + 2 * LANES), f32),
             pltpu.VMEM((1, LANES), f32),
             pltpu.VMEM((experts - 1, 1, LANES), f32),
             pltpu.VMEM((1, rows), f32),
             pltpu.VMEM((1, width), f32),
-            dma((2,)), dma((DEPTH,)), dma, dma, dma, dma, dma, dma, dma((n - 1,)),
+            dma((2,)), dma((DEPTH,)), dma, dma, dma, dma, dma, dma, dma, dma, dma((n - 1,)),
         ],
         compiler_params=pltpu.CompilerParams(
             collective_id=0, has_side_effects=True, vmem_limit_bytes=8 * 2**20

time: 23.3 us -> 22.9 us (0.983)
  Pallas kernels: 21.2 us -> 20.8 us
where the time goes in v3:
time: 22.9 us; the launch traced here: 22.7 us
  Pallas kernels  20.8 us (91%)
  between operations  1.93 us (8%)
    pallas_call x1, Pallas kernels, shards(): pl.pallas_call(functools.partial(statistics_kernel, n, experts), out_shap...  15.3 us
    pallas_call x1, Pallas kernels, shards(): pl.pallas_call(functools.partial(update_kernel, block), out_shape=[jax.Sh...  5.48 us

profile of v3, /device:TPU:0, one launch (start us, length us, event | category | flops | bytes accessed | tf_op | source)
XLA Modules:
  0.0 22.7 jit_solution(4189958195352463116)
XLA Ops:
  1.9 15.3 %statistics.1 = (f32[512,14336]{1,0:T(8,128)S(1)}, bf16[512,14336]{1,0:T(8,128)(2,1)S(1)}, f32[1,14336]{1,0:T(1,128)S(1)}, f32[1,128]{1,0:T(1,128)S(1)}, f32[1,5...) custom-call(s32[1]{0:T(128)} %bitcast.5.step_ref, f32[1]{0:T(128)} %bitcast.6.prev_ref, ...), custom_call_target="tpu_custom_call" | custom-call | tf_op jit(solution)/shard_map/statistics/pallas_call | solution.py:367
  17.3 5.5 %update.1 = (bf16[512,14336]{1,0:T(8,128)(2,1)}, f32[1,512]{1,0:T(1,128)}, f32[1,1792]{1,0:T(1,128)}, f32[1,1]{1,0:T(1,128)}) custom-call(f32[512,14336]{1,0:T(8,128)S(1)} %get-tuple-element.15.u_ref, bf16[512,14336]{1,0:T(8,128)(2,1)S(1)} %get-tuple-element.16.w_ref, f32[1,14336]{1,0:T(1,128)S(1)} %get-tuple-element.17.factor_ref, ...), custom_call_target="tpu_custom_call" | custom-call | tf_op jit(solution)/shard_map/update/pallas_call | solution.py:410
